TPU v7x, 32 devices: a whole 2x2x4 slice. The times are simulated.
32 devices in a mesh: grp: 2 (over y), row: 4 (over z), col: 4 (over x, core).
Axes of the slice: x: 2, y: 2, z: 4, core: 2. Of those that a mesh axis runs over, the one named last changes fastest.
Arguments:
- hessian_old: float32 [18432, 9216], P(('grp', 'row'), 'col'), parts along dimension 0, may hold values from -8 to 48, as said below
- tokens: bfloat16 [128, 9216], P(('grp', 'row'), 'col'), parts along dimension 0, may hold values from -6 to 6
- weight: float32 [128, 9216], P(('grp', 'row'), 'col'), parts along dimension 0, may hold values from -6 to 6
- dense_weight: float32 [128, 9216], P(('grp', 'row'), 'col'), parts along dimension 0, may hold values from -6 to 6
- block_mask: int32 [128, 72], P(('grp', 'row'), 'col'), parts along dimension 0, may hold values 0 or 1
Outputs:
- hessian: float32 [18432, 9216], P(('grp', 'row'), 'col'), parts along dimension 0
- new_weight: float32 [128, 9216], P(('grp', 'row'), 'col'), parts along dimension 0
There are 2 independent parts, one for each index of `grp`. A program takes and returns all parts, laid end to end along the dimension named above; each array names one. Nothing has to cross between parts.
Inputs may be any that keep to these rules, and one draw needn't show every extreme that they name: hessian_old is symmetric and has a positive diagonal.
All inputs are finite; a program needn't handle non-finite values. No bound on the sum of `block_mask` on one device may be relied on, other than what follows from the above.
Results may differ from a plain program's by a relative error of at most 0.0035.
Values may be sent and summed in bfloat16 or wider, within the bound.
A program may use at most 128 MiB of HBM per device.

v0:
```python
import jax
import jax.numpy as jnp
from jax import lax
from jax.sharding import PartitionSpec as P


def on_device(hessian_old, tokens, weight, dense_weight, block_mask):
    row_tile = hessian_old.shape[0]
    col_tile = hessian_old.shape[1]
    row_idx = lax.axis_index("row")
    col_idx = lax.axis_index("col")
    col_panel = lax.all_gather(tokens, "row", axis=0, tiled=True)
    features = lax.all_gather(tokens, "col", axis=1, tiled=True)
    row_panel = lax.all_to_all(features, "row", split_axis=1, concat_axis=0, tiled=True)
    gram_tile = lax.dot_general(
        row_panel, col_panel, (((0,), (0,)), ((), ())), preferred_element_type=jnp.float32
    )
    token_count = tokens.shape[0] * lax.axis_size("row")
    hessian = hessian_old + gram_tile / token_count
    row_ids = lax.broadcasted_iota(jnp.int32, (row_tile, col_tile), 0) + row_idx * row_tile
    col_ids = lax.broadcasted_iota(jnp.int32, (row_tile, col_tile), 1) + col_idx * col_tile
    local_trace = jnp.sum(jnp.where(row_ids == col_ids, hessian, jnp.float32(0.0)))
    diag_sum = lax.psum(local_trace, ("row", "col"))
    weight_rows = weight.shape[0]
    block_count = block_mask.shape[1]
    block_width = col_tile // block_count
    kept_mask = (
        block_mask.astype(jnp.float32)[:, :, None] * jnp.ones((1, 1, block_width), jnp.float32)
    ).reshape(weight_rows, col_tile)
    difference = (kept_mask * weight - dense_weight).astype(jnp.bfloat16)
    hess_low = hessian.astype(jnp.bfloat16)
    partial_grad = lax.dot_general(
        lax.all_gather(difference, "row", axis=0, tiled=True),
        hess_low,
        (((1,), (1,)), ((), ())),
        preferred_element_type=jnp.float32,
    )
    spread = lax.all_to_all(partial_grad, "row", split_axis=0, concat_axis=1, tiled=True)
    gradient = lax.psum_scatter(spread, "col", scatter_dimension=1, tiled=True)
    step_size = 0.25 * (row_tile * lax.axis_size("row")) / diag_sum
    new_weight = kept_mask * (weight - step_size * gradient)
    return (hessian, new_weight)


def solution(mesh):
    return jax.shard_map(
        on_device,
        mesh=mesh,
        in_specs=(
            P(("grp", "row"), "col"),
            P(("grp", "row"), "col"),
            P(("grp", "row"), "col"),
            P(("grp", "row"), "col"),
            P(("grp", "row"), "col"),
        ),
        out_specs=(P(("grp", "row"), "col"), P(("grp", "row"), "col")),
        check_vma=False,
    )
```

profile of v0, /device:TPU:0, one launch (start us, length us, event | category | flops | bytes accessed | tf_op | source)
XLA Modules:
  0.0 135.9 jit_solution(5965338274391581153)
XLA Ops:
  7.2 7.6 %all_gather.9 = bf16[16,9216]{1,0:T(8,128)(2,1)S(1)} all-gather(bf16[16,2304]{1,0:T(8,128)(2,1)} %param.6), channel_id=1, replica_groups=mesh['grp'=2,'row'=4,'col'=4] {'col'}, dimensions={1}, use_global_device_ids=true | all-gather | bytes 368640 | tf_op jit(solution)/shard_map/all_gather | solution.py:13
  14.8 0.7 copy.19
  15.5 4.9 %all-to-all-start = ((bf16[16,4,2304]{2,0,1:T(8,128)(2,1)}), bf16[16,4,2304]{2,0,1:T(8,128)(2,1)S(1)}, u32[]{:S(2)}, u32[]{:S(2)}) async-start(bf16[16,4,2304]{2,0,1:T(8,128)(2,1)} %bitcast.21), calls=%async_computation | async-start | bytes 589824 | tf_op jit(solution)/shard_map/all_to_all | solution.py:14
  20.4 0.0 reduce-scatter.2.cloned.1.call-start
  20.4 0.7 convert_element_type.9
  21.1 0.1 mul.23
  21.2 1.0 fusion.4
  22.2 16.3 %all_gather.10 = bf16[64,2304]{1,0:T(8,128)(2,1)S(1)} all-gather(bf16[16,2304]{1,0:T(8,128)(2,1)} %param.6), channel_id=1, replica_groups=mesh['grp'=2,'row'=4,'col'=4] {'row'}, dimensions={0}, use_global_device_ids=true | all-gather | bytes 368640 | tf_op jit(solution)/shard_map/all_gather | solution.py:12
  38.6 14.0 %all_gather.11 = bf16[64,2304]{1,0:T(8,128)(2,1)S(1)} all-gather(bf16[16,2304]{1,0:T(8,128)(2,1)S(1)} %fusion.4), channel_id=1, replica_groups=mesh['grp'=2,'row'=4,'col'=4] {'row'}, dimensions={0}, use_global_device_ids=true | all-gather | bytes 368640 | tf_op jit(solution)/shard_map/all_gather | solution.py:33
  52.5 0.0 all-to-all-done
  52.6 18.4 %select_reduce_fusion = (f32[]{:T(128)}, f32[2304,2304]{1,0:T(8,128)}) fusion(s32[2304]{0:T(1024)S(1)} %get-tuple-element.4, s32[2304]{0:T(1024)S(1)} %get-tuple-element.5, f32[2304,2304]{1,0:T(8,128)} %param.5, bf16[64,2304]{1,0:T(8,128)(2,1)S(1)} %bitcast.22, bf16[64,2304]{1,0:T(8,128)(2,1)S(1)} %all_gather.10), kind=kOutput, calls=%fused_computation.2 | convolution fusion | flops 706019328 | bytes 43075588 | tf_op jit(solution)/shard_map/dot_general | solution.py:15
  70.9 0.0 copy-start
  70.9 10.4 %fusion.1 = f32[64,2304]{1,0:T(8,128)S(1)} fusion(bf16[64,2304]{1,0:T(8,128)(2,1)S(1)} %all_gather.11, f32[2304,2304]{1,0:T(8,128)} %get-tuple-element.3), kind=kOutput, calls=%fused_computation.3 | convolution fusion | flops 684785664 | bytes 22118400 | tf_op jit(solution)/shard_map/dot_general | solution.py:32
  81.3 14.3 %all_to_all.38 = f32[4,16,2304]{2,1,0:T(8,128)S(1)} all-to-all(f32[4,16,2304]{2,1,0:T(8,128)S(1)} %bitcast.23), channel_id=1, replica_groups=mesh['grp'=2,'row'=4,'col'=4] {'row'}, dimensions={0} | all-to-all | bytes 1179648 | tf_op jit(solution)/shard_map/all_to_all | solution.py:38
  95.6 0.8 copy.14
  96.4 0.0 reduce-scatter.2.cloned.1.call-update
  96.5 30.2 %psum.7 = f32[]{:T(128)} all-reduce(f32[]{:T(128)} %get-tuple-element.2), channel_id=1, replica_groups=mesh['grp'=2,'row'=4,'col'=4] {'row','col'}, use_global_device_ids=true, to_apply=%region_1.2 | all-reduce | flops 1 | bytes 8 | tf_op jit(solution)/shard_map/psum | solution.py:23
  127.4 0.0 reduce-scatter.2.cloned.1.call-done
  127.4 0.0 copy-done
  127.4 1.6 %bitcast_multiply_fusion = f32[16,2304]{1,0:T(8,128)} fusion(f32[16,2304]{1,0:T(8,128)S(1)} %copy-done, f32[16,2304]{1,0:T(8,128)} %reduce-scatter.2.cloned.1.call-done, f32[2,8,18,128]{3,2,1,0:T(8,128)S(1)} %bitcast.27, f32[]{:T(128)S(6)} %div.11), kind=kLoop, calls=%fused_computation.6 | loop fusion | flops 110592 | bytes 589828 | tf_op jit(solution)/shard_map/mul | solution.py:41
  (1 shorter events, 0.0 us)
Async XLA Ops:
  15.5 37.0 %all-to-all-start = ((bf16[16,4,2304]{2,0,1:T(8,128)(2,1)}), bf16[16,4,2304]{2,0,1:T(8,128)(2,1)S(1)}, u32[]{:S(2)}, u32[]{:S(2)}) async-start(bf16[16,4,2304]{2,0,1:T(8,128)(2,1)} %bitcast.21), calls=%async_computation | async-start | bytes 589824 | tf_op jit(solution)/shard_map/all_to_all | solution.py:14
  20.4 107.0 %reduce-scatter.2.cloned.1.call-start = ((), (), s32[]{:S(2)}) async-start(), calls=%async_computation.3 | async-start | bytes 737280 | tf_op jit(solution)/shard_map/reduce_scatter | solution.py:39
  70.9 56.5 %copy-start = (f32[16,2304]{1,0:T(8,128)S(1)}, f32[16,2304]{1,0:T(8,128)}, u32[]{:S(2)}) copy-start(f32[16,2304]{1,0:T(8,128)} %param.7) | copy-start | bytes 442372
Sparse Core Ops, SparseCore 0:
  96.6 20.9 reduce-scatter.1
where the time goes:
time: 136 us
  blocking collectives  82.4 us (61%)
  matrix products  28.8 us (21%)
  between operations  14.8 us (11%)
  starting transfers between devices  4.87 us (4%)
  other arithmetic  3.34 us (2%)
  local copies, waits for them, and re-layouts  1.69 us (1%)
    psum x1, blocking collectives, on_device(): diag_sum = lax.psum(local_trace, ('row', 'col'))  30.2 us
    dot_general x1, matrix products, on_device(): lax.dot_general(row_panel, col_panel, (((0,), (0,)), ((), ())), preferred...  18.4 us
    all_gather x1, blocking collectives, on_device(): col_panel = lax.all_gather(tokens, 'row', axis=0, tiled=True)  16.3 us
    all_to_all x1, blocking collectives, on_device(): lax.all_to_all(partial_grad, 'row', split_axis=0, concat_axis=1, tiled=True)  14.3 us
    all_gather x1, blocking collectives, on_device(): lax.all_gather(difference, 'row', axis=0, tiled=True)  14 us
    dot_general x1, matrix products, on_device(): lax.dot_general(lax.all_gather(difference, 'row', axis=0, tiled=True), he...  10.4 us
    all_gather x1, blocking collectives, on_device(): features = lax.all_gather(tokens, 'col', axis=1, tiled=True)  7.61 us
    all_to_all x1, starting transfers between devices, on_device(): lax.all_to_all(features, 'row', split_axis=1, concat_axis=0, tiled=True)  4.87 us
  transfers between devices with their start and end apart: 2, of which 0 were waited for; matrix products, arithmetic and copies ran while one was open for 1% of the time, Pallas kernels for 0%

commit v1 on v0

--- a/solution.py
+++ b/solution.py
@@ -1,10 +1,16 @@
+import functools
+
 import jax
 import jax.numpy as jnp
 from jax import lax
+from jax.experimental import pallas as pl
+from jax.experimental.pallas import tpu as pltpu
 from jax.sharding import PartitionSpec as P
 
-
-def on_device(hessian_old, tokens, weight, dense_weight, block_mask):
+MESH = pl.DeviceIdType.MESH
+
+
+def general(hessian_old, tokens, weight, dense_weight, block_mask):
     row_tile = hessian_old.shape[0]
     col_tile = hessian_old.shape[1]
     row_idx = lax.axis_index("row")
@@ -42,17 +48,309 @@
     return (hessian, new_weight)
 
 
+def greet(devices):
+    barrier = pltpu.get_barrier_semaphore()
+    for device in devices:
+        pl.semaphore_signal(barrier, inc=1, device_id=device, device_id_type=MESH)
+    pl.semaphore_wait(barrier, len(devices))
+
+
+def remote(src, dst, send_sem, recv_sem, device):
+    return pltpu.make_async_remote_copy(
+        src_ref=src, dst_ref=dst, send_sem=send_sem, recv_sem=recv_sem,
+        device_id=device, device_id_type=MESH,
+    )
+
+
+def gather_kernel(
+    n, tok_ref, w_ref, d_ref, m_ref, colp, rowt, rowd, diff,
+    send_a, send_d, send_b, recv_a, recv_d, recv_b,
+):
+    g, r, c = lax.axis_index("grp"), lax.axis_index("row"), lax.axis_index("col")
+    blocks = m_ref.shape[1]
+    width = tok_ref.shape[1] // blocks
+    for b in range(blocks):
+        at = slice(b * width, (b + 1) * width)
+        kept = m_ref[:, b : b + 1].astype(jnp.float32)
+        diff[:, at] = (kept * w_ref[:, at] - d_ref[:, at]).astype(jnp.bfloat16)
+    others = [lax.rem(r + j, n) for j in range(1, n)]
+    beside = [lax.rem(c + j, n) for j in range(1, n)]
+    greet([(g, rr, c) for rr in others] + [(g, r, cc) for cc in beside])
+
+    root = r == c
+    partner = c + 1 - 2 * lax.rem(c, 2)
+    partner_dev = (g, r, partner)
+    twins = [(g, r, lax.rem(c + 2 * j, n)) for j in range(1, n // 2)]
+    even = lax.rem(r, 2) == lax.rem(c, 2)
+
+    def token_copy(k):
+        rr = lax.rem(c + k, n)
+        return rr, remote(tok_ref, colp.at[r], send_a.at[k], recv_a.at[r], (g, rr, c))
+
+    diff_copy = remote(diff, rowd.at[r], send_d, recv_d.at[r], (g, c, c))
+
+    @pl.when(jnp.logical_not(root))
+    def _():
+        token_copy(0)[1].start()
+        diff_copy.start()
+
+    def spread(s, token_src, diff_src, devices, start):
+        for i, device in enumerate(devices):
+            one = remote(token_src, rowt.at[s], send_b.at[i, 0, s], recv_b.at[0, s], device)
+            two = remote(diff_src, rowd.at[s], send_b.at[i, 1, s], recv_b.at[1, s], device)
+            if start:
+                one.start()
+                two.start()
+            else:
+                one.wait_send()
+                two.wait_send()
+
+    @pl.when(root)
+    def _():
+        spread(r, tok_ref, diff, twins + [partner_dev], True)
+
+    for k in range(1, n):
+        rr, copy = token_copy(k)
+
+        @pl.when(rr != r)
+        def _():
+            copy.start()
+
+    colp[r] = tok_ref[...]
+
+    def got_a(s):
+        remote(tok_ref, colp.at[s], send_a.at[0], recv_a.at[s], partner_dev).wait_recv()
+
+    def got_d(s):
+        remote(diff, rowd.at[s], send_d, recv_d.at[s], partner_dev).wait_recv()
+
+    def got_b(s):
+        remote(tok_ref, rowt.at[s], send_d, recv_b.at[0, s], partner_dev).wait_recv()
+        remote(diff, rowd.at[s], send_d, recv_b.at[1, s], partner_dev).wait_recv()
+
+    @pl.when(root)
+    def _():
+        for s in others:
+            got_a(s)
+            got_d(s)
+            spread(s, colp.at[s], rowd.at[s], twins + [partner_dev], True)
+        rowd[r] = diff[...]
+        for s in range(n):
+            rowt[s] = colp[s]
+        spread(r, tok_ref, diff, twins + [partner_dev], False)
+        for s in others:
+            spread(s, colp.at[s], rowd.at[s], twins + [partner_dev], False)
+
+    @pl.when(jnp.logical_not(root))
+    def _():
+        @pl.when(even)
+        def _():
+            for s in [r] + others:
+                got_b(s)
+                spread(s, rowt.at[s], rowd.at[s], [partner_dev], True)
+            for s in [r] + others:
+                spread(s, rowt.at[s], rowd.at[s], [partner_dev], False)
+
+        @pl.when(jnp.logical_not(even))
+        def _():
+            for s in [r] + others:
+                got_b(s)
+
+        for s in others:
+            got_a(s)
+        diff_copy.wait_send()
+
+    for k in range(n):
+        rr, copy = token_copy(k)
+
+        @pl.when(rr != r)
+        def _():
+            copy.wait_send()
+
+
+def main_kernel(n, token_count, old_ref, rt_ref, rd_ref, cp_ref, out_ref, part_ref, trace_ref, acc):
+    i = pl.program_id(0)
+    rows = old_ref.shape[0]
+
+    @pl.when(i == 0)
+    def _():
+        acc[...] = jnp.zeros_like(acc)
+        trace_ref[...] = jnp.zeros_like(trace_ref)
+
+    gram = lax.dot_general(
+        rt_ref[...], cp_ref[...], (((0,), (0,)), ((), ())), preferred_element_type=jnp.float32
+    )
+    hess = old_ref[...] + gram / token_count
+    out_ref[...] = hess
+    acc[...] += jnp.dot(rd_ref[...], hess.astype(jnp.bfloat16), preferred_element_type=jnp.float32)
+
+    @pl.when(lax.axis_index("row") == lax.axis_index("col"))
+    def _():
+        square = out_ref[:, pl.ds(pl.multiple_of(i * rows, rows), rows)]
+        same = lax.broadcasted_iota(jnp.int32, (rows, rows), 0) == lax.broadcasted_iota(
+            jnp.int32, (rows, rows), 1
+        )
+        diag = jnp.where(same, square, 0.0)
+        total = jnp.sum(diag.reshape(rows // 8, 8, rows), axis=0)
+        for b in range(rows // 128):
+            trace_ref[...] += total[:, b * 128 : (b + 1) * 128]
+
+    @pl.when(i == pl.num_programs(0) - 1)
+    def _():
+        part_ref[...] = acc[...].astype(part_ref.dtype)
+
+
+def step_kernel(n, size, part_ref, w_ref, m_ref, trace_ref, out_ref, got, traces, send_p, send_t, recv_p, recv_t):
+    g, r, c = lax.axis_index("grp"), lax.axis_index("row"), lax.axis_index("col")
+    others = [lax.rem(r + j, n) for j in range(1, n)]
+    far = [
+        (g, lax.rem(r + j, n), lax.rem(c + k, n)) for j in range(n) for k in range(n) if j or k
+    ]
+    greet(far)
+    sends = [
+        remote(part_ref.at[s], got.at[r], send_p.at[j], recv_p.at[r], (g, s, c))
+        for j, s in enumerate(others)
+    ]
+    tells = [
+        remote(trace_ref, traces.at[r], send_t.at[j], recv_t.at[r], device)
+        for j, device in enumerate(far)
+    ]
+
+    @pl.when(r == c)
+    def _():
+        for copy in tells:
+            copy.start()
+
+    for copy in sends:
+        copy.start()
+
+    total = jnp.zeros(trace_ref.shape, jnp.float32)
+    for s in range(n):
+        @pl.when(jnp.logical_or(r != c, s != r))
+        def _():
+            remote(trace_ref, traces.at[s], send_t.at[0], recv_t.at[s], far[0]).wait_recv()
+
+    @pl.when(r == c)
+    def _():
+        traces[r] = trace_ref[...]
+
+    for s in range(n):
+        total = total + traces[s]
+    step = 0.25 * size / jnp.sum(total, axis=(0, 1), keepdims=True)
+    for s in others:
+        remote(part_ref.at[0], got.at[s], send_p.at[0], recv_p.at[s], far[0]).wait_recv()
+    got[r] = part_ref[r]
+    blocks = m_ref.shape[1]
+    width = w_ref.shape[1] // blocks
+    for b in range(blocks):
+        at = slice(b * width, (b + 1) * width)
+        grad = got[0, :, at].astype(jnp.float32)
+        for s in range(1, n):
+            grad = grad + got[s, :, at].astype(jnp.float32)
+        kept = m_ref[:, b : b + 1].astype(jnp.float32)
+        out_ref[:, at] = kept * (w_ref[:, at] - step * grad)
+    for copy in sends:
+        copy.wait_send()
+
+    @pl.when(r == c)
+    def _():
+        for copy in tells:
+            copy.wait_send()
+
+
+def fused(n, hessian_old, tokens, weight, dense_weight, block_mask):
+    tile = hessian_old.shape[0]
+    held = tokens.shape[0]
+    depth = weight.shape[0]
+    vmem = pl.BlockSpec(memory_space=pltpu.VMEM)
+    dma = pltpu.SemaphoreType.DMA
+    colp, rowt, rowd = pl.pallas_call(
+        functools.partial(gather_kernel, n),
+        out_shape=(
+            jax.ShapeDtypeStruct((n, held, tile), jnp.bfloat16),
+            jax.ShapeDtypeStruct((n, held, tile), jnp.bfloat16),
+            jax.ShapeDtypeStruct((n, depth, tile), jnp.bfloat16),
+        ),
+        in_specs=[vmem] * 4,
+        out_specs=(vmem,) * 3,
+        scratch_shapes=[
+            pltpu.VMEM((depth, tile), jnp.bfloat16),
+            dma((n,)),
+            dma,
+            dma((n // 2, 2, n)),
+            dma((n,)),
+            dma((n,)),
+            dma((2, n)),
+        ],
+        compiler_params=pltpu.CompilerParams(
+            collective_id=0, has_side_effects=True, vmem_limit_bytes=8 << 20
+        ),
+    )(tokens, weight, dense_weight, block_mask)
+    colp = colp.reshape(n * held, tile)
+    rowt = rowt.reshape(n * held, tile)
+    rowd = rowd.reshape(n * depth, tile)
+    rows = 256 if tile % 256 == 0 else 128
+    hessian, partial, trace = pl.pallas_call(
+        functools.partial(main_kernel, n, n * held),
+        grid=(tile // rows,),
+        out_shape=(
+            jax.ShapeDtypeStruct((tile, tile), jnp.float32),
+            jax.ShapeDtypeStruct((n * depth, tile), jnp.bfloat16),
+            jax.ShapeDtypeStruct((8, 128), jnp.float32),
+        ),
+        in_specs=[
+            pl.BlockSpec((rows, tile), lambda i: (i, 0)),
+            pl.BlockSpec((n * held, rows), lambda i: (0, i)),
+            pl.BlockSpec((n * depth, rows), lambda i: (0, i)),
+            pl.BlockSpec((n * held, tile), lambda i: (0, 0)),
+        ],
+        out_specs=(
+            pl.BlockSpec((rows, tile), lambda i: (i, 0)),
+            pl.BlockSpec((n * depth, tile), lambda i: (0, 0)),
+            pl.BlockSpec((8, 128), lambda i: (0, 0)),
+        ),
+        scratch_shapes=[pltpu.VMEM((n * depth, tile), jnp.float32)],
+        compiler_params=pltpu.CompilerParams(vmem_limit_bytes=32 << 20),
+    )(hessian_old, rowt, rowd, colp)
+    new_weight = pl.pallas_call(
+        functools.partial(step_kernel, n, tile * n),
+        out_shape=jax.ShapeDtypeStruct((depth, tile), jnp.float32),
+        in_specs=[vmem] * 4,
+        out_specs=vmem,
+        scratch_shapes=[
+            pltpu.VMEM((n, depth, tile), jnp.bfloat16),
+            pltpu.VMEM((n, 8, 128), jnp.float32),
+            dma((n - 1,)),
+            dma((n * n - 1,)),
+            dma((n,)),
+            dma((n,)),
+        ],
+        compiler_params=pltpu.CompilerParams(
+            collective_id=1, has_side_effects=True, vmem_limit_bytes=8 << 20
+        ),
+    )(partial.reshape(n, depth, tile), weight, block_mask, trace)
+    return hessian, new_weight
+
+
 def solution(mesh):
+    n = mesh.shape["row"]
+
+    def on_device(hessian_old, tokens, weight, dense_weight, block_mask):
+        tile = hessian_old.shape[0]
+        fits = (
+            n == mesh.shape["col"]
+            and n > 1
+            and n % 2 == 0
+            and tile == hessian_old.shape[1]
+            and tile % 128 == 0
+            and tile == block_mask.shape[1] * 128
+            and tokens.shape[0] % 16 == 0
+            and weight.shape[0] % 16 == 0
+        )
+        args = (hessian_old, tokens, weight, dense_weight, block_mask)
+        return fused(n, *args) if fits else general(*args)
+
+    spec = P(("grp", "row"), "col")
     return jax.shard_map(
-        on_device,
-        mesh=mesh,
-        in_specs=(
-            P(("grp", "row"), "col"),
-            P(("grp", "row"), "col"),
-            P(("grp", "row"), "col"),
-            P(("grp", "row"), "col"),
-            P(("grp", "row"), "col"),
-        ),
-        out_specs=(P(("grp", "row"), "col"), P(("grp", "row"), "col")),
-        check_vma=False,
-    )
+        on_device, mesh=mesh, in_specs=(spec,) * 5, out_specs=(spec, spec), check_vma=False
+    )

time: 136 us -> 54.9 us (0.40)
  blocking collectives: 82.4 us -> 0 us
  Pallas kernels: 0 us -> 42.8 us
  matrix products: 28.8 us -> 0 us
  between operations: 14.8 us -> 0.67 us
  local copies, waits for them, and re-layouts: 1.69 us -> 11.1 us
  starting transfers between devices: 4.87 us -> 0 us
  other arithmetic: 3.34 us -> 0 us
    pallas_call x0 -> x3, Pallas kernels: none -> 42.8 us  [the longest x1 19.8 us: fused(): pl.pallas_call(functools.partial(gather_kernel, n), out_shape=(jax.ShapeD...]
    all_gather x3 -> x0, blocking collectives: 37.9 us -> none  [the longest x1 16.3 us: on_device(): col_panel = lax.all_gather(tokens, 'row', axis=0, tiled=True)]
    psum x1 -> x0, blocking collectives: 30.2 us -> none  [on_device(): diag_sum = lax.psum(local_trace, ('row', 'col'))]
    dot_general x2 -> x0, matrix products: 28.8 us -> none  [the longest x1 18.4 us: on_device(): lax.dot_general(row_panel, col_panel, (((0,), (0,)), ((), ())), preferred...]
    all_to_all x1 -> x0, blocking collectives: 14.3 us -> none  [on_device(): lax.all_to_all(partial_grad, 'row', split_axis=0, concat_axis=1, tiled=True)]
    unnamed x2 -> x15, local copies, waits for them, and re-layouts: 0.01 us -> 11.1 us
    all_to_all x1 -> x0, starting transfers between devices: 4.87 us -> none  [on_device(): lax.all_to_all(features, 'row', split_axis=1, concat_axis=0, tiled=True)]
    convert_element_type x2 -> x0, other arithmetic: 1.73 us -> none  [the longest x1 1.03 us: on_device(): difference = (kept_mask * weight - dense_weight).astype(jnp.bfloat16)]
  transfers between devices with their start and end apart: 2 -> 0, of which waited for: 0 -> 0; matrix products, arithmetic and copies ran while one was open for 1% -> 0% of each run, Pallas kernels for 0% -> 0%
where the time goes in v1:
time: 54.9 us; the launch traced here: 54.6 us
  Pallas kernels  42.8 us (78%)
  local copies, waits for them, and re-layouts  11.1 us (20%)
  between operations  0.67 us (1%)
    pallas_call x1, Pallas kernels, fused(): pl.pallas_call(functools.partial(gather_kernel, n), out_shape=(jax.ShapeD...  19.8 us
    pallas_call x1, Pallas kernels, fused(): pl.pallas_call(functools.partial(step_kernel, n, tile * n), out_shape=jax...  12.5 us
    unnamed x15, local copies, waits for them, and re-layouts  11.1 us
    pallas_call x1, Pallas kernels, fused(): pl.pallas_call(functools.partial(main_kernel, n, n * held), grid=(tile //...  10.5 us

profile of v1, /device:TPU:0, one launch (start us, length us, event | category | flops | bytes accessed | tf_op | source)
XLA Modules:
  0.0 54.6 jit_solution(968164981742742462)
XLA Ops:
  0.6 0.0 copy-start.1
  0.6 0.9 %copy-done.1 = f32[16,2304]{1,0:T(8,128)S(1)} copy-done((f32[16,2304]{1,0:T(8,128)S(1)}, f32[16,2304]{1,0:T(8,128)}, u32[]{:S(2)}) %copy-start.1) | copy-done | bytes 147480
  1.5 0.0 copy-start.3
  1.5 0.9 %copy-done.3 = f32[16,2304]{1,0:T(8,128)S(1)} copy-done((f32[16,2304]{1,0:T(8,128)S(1)}, f32[16,2304]{1,0:T(8,128)}, u32[]{:S(2)}) %copy-start.3) | copy-done | bytes 147480
  2.5 0.0 copy-start.4
  2.5 0.9 %copy-done.4 = bf16[16,2304]{1,0:T(8,128)(2,1)S(1)} copy-done((bf16[16,2304]{1,0:T(8,128)(2,1)S(1)}, bf16[16,2304]{1,0:T(8,128)(2,1)}, u32[]{:S(2)}) %copy-start.4) | copy-done | bytes 73752
  3.3 0.0 copy-start.5
  3.3 0.7 %copy-done.5 = s32[16,18]{1,0:T(8,128)S(1)} copy-done((s32[16,18]{1,0:T(8,128)S(1)}, s32[16,18]{1,0:T(8,128)}, u32[]{:S(2)}) %copy-start.5) | copy-done | bytes 1176
  4.0 0.0 copy-start.2
  4.0 0.0 copy-start.6
  4.0 19.8 %shard_map.68 = (bf16[4,16,2304]{2,1,0:T(8,128)(2,1)S(1)}, bf16[4,16,2304]{2,1,0:T(8,128)(2,1)S(1)}, bf16[4,16,2304]{2,1,0:T(8,128)(2,1)S(1)}) custom-call(bf16[16,2304]{1,0:T(8,128)(2,1)S(1)} %copy-done.4, f32[16,2304]{1,0:T(8,128)S(1)} %copy-done.1, f32[16,2304]{1,0:T(8,128)S(1)} %copy-done.3, s32[16,18]{1,0:T(8,128)S(1)} %copy-done.5), custom_call_target="tpu_custom_call" | custom-call | tf_op jit(solution)/shard_map/pallas_call | solution.py:267
  23.8 0.0 copy-start
  23.9 7.0 %copy-done = f32[2304,2304]{1,0:T(8,128)S(1)} copy-done((f32[2304,2304]{1,0:T(8,128)S(1)}, f32[2304,2304]{1,0:T(8,128)}, u32[]{:S(2)}) %copy-start) | copy-done | bytes 21233688
  30.9 10.5 %shard_map.69 = (f32[2304,2304]{1,0:T(8,128)}, bf16[64,2304]{1,0:T(8,128)(2,1)S(1)}, f32[8,128]{1,0:T(8,128)S(1)}) custom-call(f32[2304,2304]{1,0:T(8,128)S(1)} %copy-done, bf16[64,2304]{1,0:T(8,128)(2,1)S(1)} %bitcast.6, bf16[64,2304]{1,0:T(8,128)(2,1)S(1)} %bitcast.7, bf16[64,2304]{1,0:T(8,128)(2,1)S(1)} %bitcast.5), custom_call_target="tpu_custom_call" | custom-call | tf_op jit(solution)/shard_map/pallas_call | solution.py:293
  41.4 0.0 copy-done.2
  41.4 0.0 copy-done.6
  41.4 12.5 %shard_map.70 = f32[16,2304]{1,0:T(8,128)S(1)} custom-call(bf16[4,16,2304]{2,1,0:T(8,128)(2,1)S(1)} %bitcast.4, f32[16,2304]{1,0:T(8,128)S(1)} %copy-done.2, s32[16,18]{1,0:T(8,128)S(1)} %copy-done.6, f32[8,128]{1,0:T(8,128)S(1)} %get-tuple-element.13.trace_ref), custom_call_target="tpu_custom_call" | custom-call | tf_op jit(solution)/shard_map/pallas_call | solution.py:315
  54.0 0.7 %copy.8 = f32[16,2304]{1,0:T(8,128)} copy(f32[16,2304]{1,0:T(8,128)S(1)} %shard_map.70) | data formatting | bytes 294912
Async XLA Ops:
  0.6 0.9 %copy-start.1 = (f32[16,2304]{1,0:T(8,128)S(1)}, f32[16,2304]{1,0:T(8,128)}, u32[]{:S(2)}) copy-start(f32[16,2304]{1,0:T(8,128)} %w_ref.3) | copy-start | bytes 442372
  1.5 0.9 %copy-start.3 = (f32[16,2304]{1,0:T(8,128)S(1)}, f32[16,2304]{1,0:T(8,128)}, u32[]{:S(2)}) copy-start(f32[16,2304]{1,0:T(8,128)} %d_ref.1) | copy-start | bytes 442372
  2.5 0.9 %copy-start.4 = (bf16[16,2304]{1,0:T(8,128)(2,1)S(1)}, bf16[16,2304]{1,0:T(8,128)(2,1)}, u32[]{:S(2)}) copy-start(bf16[16,2304]{1,0:T(8,128)(2,1)} %tok_ref.1) | copy-start | bytes 221188
  3.3 0.7 %copy-start.5 = (s32[16,18]{1,0:T(8,128)S(1)}, s32[16,18]{1,0:T(8,128)}, u32[]{:S(2)}) copy-start(s32[16,18]{1,0:T(8,128)} %m_ref.3) | copy-start | bytes 3460
  4.0 37.4 %copy-start.2 = (f32[16,2304]{1,0:T(8,128)S(1)}, f32[16,2304]{1,0:T(8,128)}, u32[]{:S(2)}) copy-start(f32[16,2304]{1,0:T(8,128)} %w_ref.3) | copy-start | bytes 442372
  4.0 37.4 %copy-start.6 = (s32[16,18]{1,0:T(8,128)S(1)}, s32[16,18]{1,0:T(8,128)}, u32[]{:S(2)}) copy-start(s32[16,18]{1,0:T(8,128)} %m_ref.3) | copy-start | bytes 3460
  23.8 7.0 %copy-start = (f32[2304,2304]{1,0:T(8,128)S(1)}, f32[2304,2304]{1,0:T(8,128)}, u32[]{:S(2)}) copy-start(f32[2304,2304]{1,0:T(8,128)} %old_ref.1) | copy-start | bytes 63700996

commit v2 on v1

--- a/solution.py
+++ b/solution.py
@@ -48,11 +48,14 @@
     return (hessian, new_weight)
 
 
-def greet(devices):
+def hail(devices):
     barrier = pltpu.get_barrier_semaphore()
     for device in devices:
         pl.semaphore_signal(barrier, inc=1, device_id=device, device_id_type=MESH)
-    pl.semaphore_wait(barrier, len(devices))
+
+
+def meet(count):
+    pl.semaphore_wait(pltpu.get_barrier_semaphore(), count)
 
 
 def remote(src, dst, send_sem, recv_sem, device):
@@ -63,19 +66,30 @@
 
 
 def gather_kernel(
-    n, tok_ref, w_ref, d_ref, m_ref, colp, rowt, rowd, diff,
-    send_a, send_d, send_b, recv_a, recv_d, recv_b,
+    n, old_hbm, tok_hbm, w_hbm, d_hbm, m_hbm, old, colp, rowt, rowd, tok_ref, w_ref, d_ref, m_ref, diff,
+    in_sem, send_a, send_d, send_b, recv_a, recv_d, recv_b,
 ):
     g, r, c = lax.axis_index("grp"), lax.axis_index("row"), lax.axis_index("col")
+    loads = [
+        pltpu.make_async_copy(src, dst, in_sem.at[i])
+        for i, (src, dst) in enumerate(
+            [(w_hbm, w_ref), (d_hbm, d_ref), (m_hbm, m_ref), (tok_hbm, tok_ref), (old_hbm, old)]
+        )
+    ]
+    for load in loads:
+        load.start()
+    others = [lax.rem(r + j, n) for j in range(1, n)]
+    beside = [lax.rem(c + j, n) for j in range(1, n)]
+    hail([(g, rr, c) for rr in others] + [(g, r, cc) for cc in beside])
+    for load in loads[:4]:
+        load.wait()
     blocks = m_ref.shape[1]
     width = tok_ref.shape[1] // blocks
     for b in range(blocks):
         at = slice(b * width, (b + 1) * width)
         kept = m_ref[:, b : b + 1].astype(jnp.float32)
         diff[:, at] = (kept * w_ref[:, at] - d_ref[:, at]).astype(jnp.bfloat16)
-    others = [lax.rem(r + j, n) for j in range(1, n)]
-    beside = [lax.rem(c + j, n) for j in range(1, n)]
-    greet([(g, rr, c) for rr in others] + [(g, r, cc) for cc in beside])
+    meet(len(others) + len(beside))
 
     root = r == c
     partner = c + 1 - 2 * lax.rem(c, 2)
@@ -167,37 +181,57 @@
         def _():
             copy.wait_send()
 
-
-def main_kernel(n, token_count, old_ref, rt_ref, rd_ref, cp_ref, out_ref, part_ref, trace_ref, acc):
-    i = pl.program_id(0)
-    rows = old_ref.shape[0]
-
-    @pl.when(i == 0)
-    def _():
-        acc[...] = jnp.zeros_like(acc)
-        trace_ref[...] = jnp.zeros_like(trace_ref)
-
-    gram = lax.dot_general(
-        rt_ref[...], cp_ref[...], (((0,), (0,)), ((), ())), preferred_element_type=jnp.float32
-    )
-    hess = old_ref[...] + gram / token_count
-    out_ref[...] = hess
-    acc[...] += jnp.dot(rd_ref[...], hess.astype(jnp.bfloat16), preferred_element_type=jnp.float32)
-
-    @pl.when(lax.axis_index("row") == lax.axis_index("col"))
-    def _():
-        square = out_ref[:, pl.ds(pl.multiple_of(i * rows, rows), rows)]
-        same = lax.broadcasted_iota(jnp.int32, (rows, rows), 0) == lax.broadcasted_iota(
-            jnp.int32, (rows, rows), 1
-        )
-        diag = jnp.where(same, square, 0.0)
-        total = jnp.sum(diag.reshape(rows // 8, 8, rows), axis=0)
-        for b in range(rows // 128):
-            trace_ref[...] += total[:, b * 128 : (b + 1) * 128]
-
-    @pl.when(i == pl.num_programs(0) - 1)
-    def _():
-        part_ref[...] = acc[...].astype(part_ref.dtype)
+    loads[4].wait()
+
+
+def main_kernel(
+    n, rows, token_count, old_ref, rt_ref, rd_ref, cp_ref, out_hbm, part_ref, trace_ref, acc, out, out_sem
+):
+    tile = old_ref.shape[0]
+    steps = tile // rows
+    slots = out.shape[0]
+    acc[...] = jnp.zeros_like(acc)
+    trace_ref[...] = jnp.zeros_like(trace_ref)
+    same = lax.broadcasted_iota(jnp.int32, (rows, rows), 0) == lax.broadcasted_iota(
+        jnp.int32, (rows, rows), 1
+    )
+
+    def store(i):
+        return pltpu.make_async_copy(
+            out.at[lax.rem(i, slots)],
+            out_hbm.at[pl.ds(pl.multiple_of(i * rows, rows), rows), :],
+            out_sem.at[lax.rem(i, slots)],
+        )
+
+    @pl.loop(0, steps)
+    def _(i):
+        slot = lax.rem(i, slots)
+
+        @pl.when(i >= slots)
+        def _():
+            store(i - slots).wait()
+
+        here = pl.ds(pl.multiple_of(i * rows, rows), rows)
+        gram = lax.dot_general(
+            rt_ref[:, here], cp_ref[...], (((0,), (0,)), ((), ())), preferred_element_type=jnp.float32
+        )
+        hess = old_ref[here, :] + gram / token_count
+        out[slot] = hess
+        acc[...] += jnp.dot(
+            rd_ref[:, here], hess.astype(jnp.bfloat16), preferred_element_type=jnp.float32
+        )
+        store(i).start()
+
+        @pl.when(lax.axis_index("row") == lax.axis_index("col"))
+        def _():
+            diag = jnp.where(same, out[slot, :, here], 0.0)
+            total = jnp.sum(diag.reshape(rows // 8, 8, rows), axis=0)
+            for b in range(rows // 128):
+                trace_ref[...] += total[:, b * 128 : (b + 1) * 128]
+
+    part_ref[...] = acc[...].astype(part_ref.dtype)
+    for k in range(min(slots, steps)):
+        store(jnp.int32(steps - 1 - k)).wait()
 
 
 def step_kernel(n, size, part_ref, w_ref, m_ref, trace_ref, out_ref, got, traces, send_p, send_t, recv_p, recv_t):
@@ -206,7 +240,8 @@
     far = [
         (g, lax.rem(r + j, n), lax.rem(c + k, n)) for j in range(n) for k in range(n) if j or k
     ]
-    greet(far)
+    hail(far)
+    meet(len(far))
     sends = [
         remote(part_ref.at[s], got.at[r], send_p.at[j], recv_p.at[r], (g, s, c))
         for j, s in enumerate(others)
@@ -264,17 +299,24 @@
     depth = weight.shape[0]
     vmem = pl.BlockSpec(memory_space=pltpu.VMEM)
     dma = pltpu.SemaphoreType.DMA
-    colp, rowt, rowd = pl.pallas_call(
+    hbm = pl.BlockSpec(memory_space=pltpu.HBM)
+    old, colp, rowt, rowd = pl.pallas_call(
         functools.partial(gather_kernel, n),
         out_shape=(
+            jax.ShapeDtypeStruct((tile, tile), jnp.float32),
             jax.ShapeDtypeStruct((n, held, tile), jnp.bfloat16),
             jax.ShapeDtypeStruct((n, held, tile), jnp.bfloat16),
             jax.ShapeDtypeStruct((n, depth, tile), jnp.bfloat16),
         ),
-        in_specs=[vmem] * 4,
-        out_specs=(vmem,) * 3,
+        in_specs=[hbm] * 5,
+        out_specs=(vmem,) * 4,
         scratch_shapes=[
+            pltpu.VMEM((held, tile), jnp.bfloat16),
+            pltpu.VMEM((depth, tile), jnp.float32),
+            pltpu.VMEM((depth, tile), jnp.float32),
+            pltpu.VMEM(block_mask.shape, jnp.int32),
             pltpu.VMEM((depth, tile), jnp.bfloat16),
+            dma((5,)),
             dma((n,)),
             dma,
             dma((n // 2, 2, n)),
@@ -283,35 +325,29 @@
             dma((2, n)),
         ],
         compiler_params=pltpu.CompilerParams(
-            collective_id=0, has_side_effects=True, vmem_limit_bytes=8 << 20
+            collective_id=0, has_side_effects=True, vmem_limit_bytes=4 << 20
         ),
-    )(tokens, weight, dense_weight, block_mask)
+    )(*[pltpu.with_memory_space_constraint(x, pltpu.HBM) for x in (hessian_old, tokens, weight, dense_weight, block_mask)])
     colp = colp.reshape(n * held, tile)
     rowt = rowt.reshape(n * held, tile)
     rowd = rowd.reshape(n * depth, tile)
-    rows = 256 if tile % 256 == 0 else 128
+    rows = 128
     hessian, partial, trace = pl.pallas_call(
-        functools.partial(main_kernel, n, n * held),
-        grid=(tile // rows,),
+        functools.partial(main_kernel, n, rows, n * held),
         out_shape=(
             jax.ShapeDtypeStruct((tile, tile), jnp.float32),
             jax.ShapeDtypeStruct((n * depth, tile), jnp.bfloat16),
             jax.ShapeDtypeStruct((8, 128), jnp.float32),
         ),
-        in_specs=[
-            pl.BlockSpec((rows, tile), lambda i: (i, 0)),
-            pl.BlockSpec((n * held, rows), lambda i: (0, i)),
-            pl.BlockSpec((n * depth, rows), lambda i: (0, i)),
-            pl.BlockSpec((n * held, tile), lambda i: (0, 0)),
+        in_specs=[vmem] * 4,
+        out_specs=(hbm, vmem, vmem),
+        scratch_shapes=[
+            pltpu.VMEM((n * depth, tile), jnp.float32),
+            pltpu.VMEM((4, rows, tile), jnp.float32),
+            dma((4,)),
         ],
-        out_specs=(
-            pl.BlockSpec((rows, tile), lambda i: (i, 0)),
-            pl.BlockSpec((n * depth, tile), lambda i: (0, 0)),
-            pl.BlockSpec((8, 128), lambda i: (0, 0)),
-        ),
-        scratch_shapes=[pltpu.VMEM((n * depth, tile), jnp.float32)],
-        compiler_params=pltpu.CompilerParams(vmem_limit_bytes=32 << 20),
-    )(hessian_old, rowt, rowd, colp)
+        compiler_params=pltpu.CompilerParams(vmem_limit_bytes=12 << 20),
+    )(old, rowt, rowd, colp)
     new_weight = pl.pallas_call(
         functools.partial(step_kernel, n, tile * n),
         out_shape=jax.ShapeDtypeStruct((depth, tile), jnp.float32),

time: 54.9 us -> 44 us (0.80)
  local copies, waits for them, and re-layouts: 11.1 us -> 0.67 us
    unnamed x15 -> x5, local copies, waits for them, and re-layouts: 11.1 us -> 0.67 us
where the time goes in v2:
time: 44 us; the launch traced here: 43.9 us
  Pallas kernels  42.5 us (97%)
  between operations  0.69 us (2%)
  local copies, waits for them, and re-layouts  0.67 us (2%)
    pallas_call x1, Pallas kernels, fused(): pl.pallas_call(functools.partial(gather_kernel, n), out_shape=(jax.ShapeD...  19.8 us
    pallas_call x1, Pallas kernels, fused(): pl.pallas_call(functools.partial(step_kernel, n, tile * n), out_shape=jax...  12.5 us
    pallas_call x1, Pallas kernels, fused(): pl.pallas_call(functools.partial(main_kernel, n, rows, n * held), out_sha...  10.2 us

profile of v2, /device:TPU:0, one launch (start us, length us, event | category | flops | bytes accessed | tf_op | source)
XLA Modules:
  0.0 43.9 jit_solution(10499727642879225677)
XLA Ops:
  0.6 0.0 copy-start.1
  0.6 0.0 copy-start
  0.7 19.8 %shard_map.68 = (f32[2304,2304]{1,0:T(8,128)S(1)}, bf16[4,16,2304]{2,1,0:T(8,128)(2,1)S(1)}, bf16[4,16,2304]{2,1,0:T(8,128)(2,1)S(1)}, bf16[4,16,2304]{2,1,0:T(8,128)(2,1)S(1)}) custom-call(f32[2304,2304]{1,0:T(8,128)} %old_hbm.1, bf16[16,2304]{1,0:T(8,128)(2,1)} %tok_hbm.1, f32[16,2304]{1,0:T(8,128)} %w_ref.1, f32[16,2304]{1,0:T(8,128)} %d_hbm.1, ...), custom_call_target="tpu_custom_call" | custom-call | tf_op jit(solution)/shard_map/pallas_call | solution.py:303
  20.4 10.2 %shard_map.69 = (f32[2304,2304]{1,0:T(8,128)}, bf16[64,2304]{1,0:T(8,128)(2,1)S(1)}, f32[8,128]{1,0:T(8,128)S(1)}) custom-call(f32[2304,2304]{1,0:T(8,128)S(1)} %get-tuple-element.9.old_ref, bf16[64,2304]{1,0:T(8,128)(2,1)S(1)} %bitcast.6, bf16[64,2304]{1,0:T(8,128)(2,1)S(1)} %bitcast.7, bf16[64,2304]{1,0:T(8,128)(2,1)S(1)} %bitcast.5), custom_call_target="tpu_custom_call" | custom-call | tf_op jit(solution)/shard_map/pallas_call | solution.py:335
  30.7 0.0 copy-done.1
  30.7 0.0 copy-done
  30.7 12.5 %shard_map.70 = f32[16,2304]{1,0:T(8,128)S(1)} custom-call(bf16[4,16,2304]{2,1,0:T(8,128)(2,1)S(1)} %bitcast.4, f32[16,2304]{1,0:T(8,128)S(1)} %copy-done, s32[16,18]{1,0:T(8,128)S(1)} %copy-done.1, f32[8,128]{1,0:T(8,128)S(1)} %get-tuple-element.15.trace_ref), custom_call_target="tpu_custom_call" | custom-call | tf_op jit(solution)/shard_map/pallas_call | solution.py:351
  43.2 0.7 %copy.8 = f32[16,2304]{1,0:T(8,128)} copy(f32[16,2304]{1,0:T(8,128)S(1)} %shard_map.70) | data formatting | bytes 294912
Async XLA Ops:
  0.6 30.0 %copy-start.1 = (s32[16,18]{1,0:T(8,128)S(1)}, s32[16,18]{1,0:T(8,128)}, u32[]{:S(2)}) copy-start(s32[16,18]{1,0:T(8,128)} %m_ref.1) | copy-start | bytes 3460
  0.6 30.0 %copy-start = (f32[16,2304]{1,0:T(8,128)S(1)}, f32[16,2304]{1,0:T(8,128)}, u32[]{:S(2)}) copy-start(f32[16,2304]{1,0:T(8,128)} %w_ref.1) | copy-start | bytes 442372

commit v3 on v2

--- a/solution.py
+++ b/solution.py
@@ -67,7 +67,7 @@
 
 def gather_kernel(
     n, old_hbm, tok_hbm, w_hbm, d_hbm, m_hbm, old, colp, rowt, rowd, tok_ref, w_ref, d_ref, m_ref, diff,
-    in_sem, send_a, send_d, send_b, recv_a, recv_d, recv_b,
+    in_sem, send_a, send_d, send_b, send_r, recv_a, recv_d, recv_b,
 ):
     g, r, c = lax.axis_index("grp"), lax.axis_index("row"), lax.axis_index("col")
     loads = [
@@ -97,6 +97,17 @@
     twins = [(g, r, lax.rem(c + 2 * j, n)) for j in range(1, n // 2)]
     even = lax.rem(r, 2) == lax.rem(c, 2)
 
+    mate = partner
+    crosses = r // 2 != c // 2
+
+    def direct(rr):
+        return jnp.logical_and(rr != r, jnp.logical_not(jnp.logical_and(crosses, rr == mate)))
+
+    def relay(s):
+        return s // 2 != r // 2, remote(
+            colp.at[s], colp.at[s], send_r.at[s], recv_a.at[s], (g, mate, c)
+        )
+
     def token_copy(k):
         rr = lax.rem(c + k, n)
         return rr, remote(tok_ref, colp.at[r], send_a.at[k], recv_a.at[r], (g, rr, c))
@@ -126,7 +137,7 @@
     for k in range(1, n):
         rr, copy = token_copy(k)
 
-        @pl.when(rr != r)
+        @pl.when(direct(rr))
         def _():
             copy.start()
 
@@ -148,12 +159,24 @@
             got_a(s)
             got_d(s)
             spread(s, colp.at[s], rowd.at[s], twins + [partner_dev], True)
+            far, copy = relay(s)
+
+            @pl.when(far)
+            def _():
+                copy.start()
+
         rowd[r] = diff[...]
         for s in range(n):
             rowt[s] = colp[s]
         spread(r, tok_ref, diff, twins + [partner_dev], False)
         for s in others:
             spread(s, colp.at[s], rowd.at[s], twins + [partner_dev], False)
+            far, copy = relay(s)
+
+            @pl.when(far)
+            def _():
+                copy.wait_send()
+
 
     @pl.when(jnp.logical_not(root))
     def _():
@@ -177,11 +200,16 @@
     for k in range(n):
         rr, copy = token_copy(k)
 
-        @pl.when(rr != r)
+        @pl.when(direct(rr))
         def _():
             copy.wait_send()
 
     loads[4].wait()
+
+
+def scaled(value, count):
+    exact = count & (count - 1) == 0
+    return value * (1.0 / count) if exact else value / count
 
 
 def main_kernel(
@@ -215,7 +243,7 @@
         gram = lax.dot_general(
             rt_ref[:, here], cp_ref[...], (((0,), (0,)), ((), ())), preferred_element_type=jnp.float32
         )
-        hess = old_ref[here, :] + gram / token_count
+        hess = old_ref[here, :] + scaled(gram, token_count)
         out[slot] = hess
         acc[...] += jnp.dot(
             rd_ref[:, here], hess.astype(jnp.bfloat16), preferred_element_type=jnp.float32
@@ -322,6 +350,7 @@
             dma((n // 2, 2, n)),
             dma((n,)),
             dma((n,)),
+            dma((n,)),
             dma((2, n)),
         ],
         compiler_params=pltpu.CompilerParams(
@@ -331,7 +360,7 @@
     colp = colp.reshape(n * held, tile)
     rowt = rowt.reshape(n * held, tile)
     rowd = rowd.reshape(n * depth, tile)
-    rows = 128
+    rows = 256 if tile % 256 == 0 else 128
     hessian, partial, trace = pl.pallas_call(
         functools.partial(main_kernel, n, rows, n * held),
         out_shape=(
@@ -343,10 +372,10 @@
         out_specs=(hbm, vmem, vmem),
         scratch_shapes=[
             pltpu.VMEM((n * depth, tile), jnp.float32),
-            pltpu.VMEM((4, rows, tile), jnp.float32),
-            dma((4,)),
+            pltpu.VMEM((3, rows, tile), jnp.float32),
+            dma((3,)),
         ],
-        compiler_params=pltpu.CompilerParams(vmem_limit_bytes=12 << 20),
+        compiler_params=pltpu.CompilerParams(vmem_limit_bytes=16 << 20),
     )(old, rowt, rowd, colp)
     new_weight = pl.pallas_call(
         functools.partial(step_kernel, n, tile * n),

time: 44 us -> 39.6 us (0.900)
  Pallas kernels: 42.5 us -> 38.1 us
    pallas_call x1, Pallas kernels: 10.2 us -> 7.87 us  [fused(): pl.pallas_call(functools.partial(main_kernel, n, rows, n * held), out_sha...]
    pallas_call x1, Pallas kernels: 19.8 us -> 17.6 us  [fused(): pl.pallas_call(functools.partial(gather_kernel, n), out_shape=(jax.ShapeD...]
where the time goes in v3:
time: 39.6 us; the launch traced here: 39.5 us
  Pallas kernels  38.1 us (96%)
  between operations  0.69 us (2%)
  local copies, waits for them, and re-layouts  0.67 us (2%)
    pallas_call x1, Pallas kernels, fused(): pl.pallas_call(functools.partial(gather_kernel, n), out_shape=(jax.ShapeD...  17.6 us
    pallas_call x1, Pallas kernels, fused(): pl.pallas_call(functools.partial(step_kernel, n, tile * n), out_shape=jax...  12.7 us
    pallas_call x1, Pallas kernels, fused(): pl.pallas_call(functools.partial(main_kernel, n, rows, n * held), out_sha...  7.87 us

profile of v3, /device:TPU:0, one launch (start us, length us, event | category | flops | bytes accessed | tf_op | source)
XLA Modules:
  0.0 39.5 jit_solution(12782383497921203903)
XLA Ops:
  0.6 0.0 copy-start.1
  0.6 0.0 copy-start
  0.7 17.6 %shard_map.68 = (f32[2304,2304]{1,0:T(8,128)S(1)}, bf16[4,16,2304]{2,1,0:T(8,128)(2,1)S(1)}, bf16[4,16,2304]{2,1,0:T(8,128)(2,1)S(1)}, bf16[4,16,2304]{2,1,0:T(8,128)(2,1)S(1)}) custom-call(f32[2304,2304]{1,0:T(8,128)} %old_hbm.1, bf16[16,2304]{1,0:T(8,128)(2,1)} %tok_hbm.1, f32[16,2304]{1,0:T(8,128)} %w_ref.1, f32[16,2304]{1,0:T(8,128)} %d_hbm.1, ...), custom_call_target="tpu_custom_call" | custom-call | tf_op jit(solution)/shard_map/pallas_call | solution.py:331
  18.2 7.9 %shard_map.69 = (f32[2304,2304]{1,0:T(8,128)}, bf16[64,2304]{1,0:T(8,128)(2,1)S(1)}, f32[8,128]{1,0:T(8,128)S(1)}) custom-call(f32[2304,2304]{1,0:T(8,128)S(1)} %get-tuple-element.9.old_ref, bf16[64,2304]{1,0:T(8,128)(2,1)S(1)} %bitcast.6, bf16[64,2304]{1,0:T(8,128)(2,1)S(1)} %bitcast.7, bf16[64,2304]{1,0:T(8,128)(2,1)S(1)} %bitcast.5), custom_call_target="tpu_custom_call" | custom-call | tf_op jit(solution)/shard_map/pallas_call | solution.py:364
  26.1 0.0 copy-done.1
  26.1 0.0 copy-done
  26.1 12.7 %shard_map.70 = f32[16,2304]{1,0:T(8,128)S(1)} custom-call(bf16[4,16,2304]{2,1,0:T(8,128)(2,1)S(1)} %bitcast.4, f32[16,2304]{1,0:T(8,128)S(1)} %copy-done, s32[16,18]{1,0:T(8,128)S(1)} %copy-done.1, f32[8,128]{1,0:T(8,128)S(1)} %get-tuple-element.15.trace_ref), custom_call_target="tpu_custom_call" | custom-call | tf_op jit(solution)/shard_map/pallas_call | solution.py:380
  38.8 0.7 %copy.8 = f32[16,2304]{1,0:T(8,128)} copy(f32[16,2304]{1,0:T(8,128)S(1)} %shard_map.70) | data formatting | bytes 294912
Async XLA Ops:
  0.6 25.5 %copy-start.1 = (s32[16,18]{1,0:T(8,128)S(1)}, s32[16,18]{1,0:T(8,128)}, u32[]{:S(2)}) copy-start(s32[16,18]{1,0:T(8,128)} %m_ref.1) | copy-start | bytes 3460
  0.6 25.5 %copy-start = (f32[16,2304]{1,0:T(8,128)S(1)}, f32[16,2304]{1,0:T(8,128)}, u32[]{:S(2)}) copy-start(f32[16,2304]{1,0:T(8,128)} %w_ref.1) | copy-start | bytes 442372
